TPU v7x, 64 devices: a 2x2x8 block of a 4x4x8 slice. The times are simulated.
64 devices in a mesh: rep: 4 (over x, y), g: 16 (over z, core).
Axes of the slice: x: 2, y: 2, z: 8, core: 2. Of those that a mesh axis runs over, the one named last changes fastest.
The devices are a block of a 4x4x8 slice.
Arguments:
- hidden: bfloat16 [2048, 2048], P(('rep', 'g')), parts along dimension 0
- cache_lat: bfloat16 [2048, 512, 512], P(('rep', 'g')), parts along dimension 0
- cache_rope: bfloat16 [2048, 512, 64], P(('rep', 'g')), parts along dimension 0
- seq_lens: int32 [2048], P(('rep', 'g')), parts along dimension 0
- gain_attn: bfloat16 [2048], replicated
- w_dq: bfloat16 [2048, 768], replicated
- gain_q: bfloat16 [768], replicated
- w_uq: bfloat16 [768, 20, 192], replicated
- w_qr: bfloat16 [768, 20, 64], replicated
- w_dkv: bfloat16 [2048, 576], replicated
- gain_kv: bfloat16 [512], replicated
- w_uk: bfloat16 [512, 20, 192], replicated
- w_uv: bfloat16 [512, 20, 256], replicated
- w_o: bfloat16 [5120, 2048], replicated
- gain_mlp: bfloat16 [2048], replicated
- w_gate: bfloat16 [2048, 10240], P(None, 'g')
- w_up: bfloat16 [2048, 10240], P(None, 'g')
- w_down: bfloat16 [10240, 2048], P('g')
Outputs:
- output 1: bfloat16 [2048, 2048], P(('rep', 'g')), parts along dimension 0
- output 2: bfloat16 [2048, 512], P(('rep', 'g')), parts along dimension 0
- output 3: bfloat16 [2048, 64], P(('rep', 'g')), parts along dimension 0
There are 4 independent parts. A program takes and returns all parts, laid end to end along the dimension named above; an argument that names none is the same for every part.
All inputs are finite; a program needn't handle non-finite values.
Results may differ from a plain program's by a relative error of at most 0.013522.
Values are sent between devices in bfloat16 or wider.
A program may use at most 768 MiB of HBM per device.

v0:
```python
import jax
import jax.numpy as jnp
from jax import lax
from jax.sharding import PartitionSpec as P


def rms_norm(values, gain_vec):
    mean_sq = jnp.mean(jnp.square(values), axis=-1, keepdims=True)
    return values * lax.rsqrt(mean_sq + 1e-6) * gain_vec.astype(jnp.float32)


def apply_rope(values, positions):
    half_dim = values.shape[-1] // 2
    inv_freq = 10000.0 ** (-jnp.arange(half_dim).astype(jnp.float32) / half_dim)
    angles = positions.astype(jnp.float32)[..., None] * inv_freq
    cos_part = jnp.cos(angles)
    sin_part = jnp.sin(angles)
    first_half = values[..., :half_dim]
    second_half = values[..., half_dim:]
    return jnp.concatenate([first_half * cos_part - second_half * sin_part, first_half * sin_part + second_half * cos_part], axis=-1)


def attention_rows(hidden, cache_lat, cache_rope, seq_lens, gain_attn, w_dq, gain_q, w_uq, w_qr, w_dkv, gain_kv, w_uk, w_uv, w_o):
    kv_dim = w_uk.shape[0]
    cache_len = cache_lat.shape[1]
    score_scale = (w_uq.shape[2] + w_qr.shape[2]) ** -0.5
    normed = rms_norm(hidden.astype(jnp.float32), gain_attn).astype(jnp.bfloat16)
    q_in = rms_norm(jnp.dot(normed, w_dq, preferred_element_type=jnp.float32), gain_q).astype(jnp.bfloat16)
    q_nope = jnp.einsum("bq,qhn->bhn", q_in, w_uq, preferred_element_type=jnp.float32).astype(jnp.bfloat16)
    q_rope = apply_rope(jnp.einsum("bq,qhr->bhr", q_in, w_qr, preferred_element_type=jnp.float32), seq_lens[:, None]).astype(jnp.bfloat16)
    kv_raw = jnp.dot(normed, w_dkv, preferred_element_type=jnp.float32)
    new_lat = rms_norm(kv_raw[:, :kv_dim], gain_kv).astype(jnp.bfloat16)
    new_rope = apply_rope(kv_raw[:, kv_dim:], seq_lens).astype(jnp.bfloat16)
    q_abs = jnp.einsum("bhn,chn->bhc", q_nope, w_uk, preferred_element_type=jnp.float32).astype(jnp.bfloat16)
    past_score = (jnp.einsum("bhc,blc->bhl", q_abs, cache_lat, preferred_element_type=jnp.float32) + jnp.einsum("bhr,blr->bhl", q_rope, cache_rope, preferred_element_type=jnp.float32)) * score_scale
    own_score = (jnp.einsum("bhc,bc->bh", q_abs, new_lat, preferred_element_type=jnp.float32) + jnp.einsum("bhr,br->bh", q_rope, new_rope, preferred_element_type=jnp.float32)) * score_scale
    key_pos = lax.broadcasted_iota(jnp.int32, (1, 1, cache_len), 2)
    past_score = jnp.where(key_pos < seq_lens[:, None, None], past_score, -jnp.inf)
    row_max = jnp.maximum(jnp.max(past_score, axis=-1), own_score)
    past_exp = jnp.exp(past_score - row_max[..., None])
    own_exp = jnp.exp(own_score - row_max)
    row_total = jnp.sum(past_exp, axis=-1) + own_exp
    past_prob = (past_exp / row_total[..., None]).astype(jnp.bfloat16)
    own_prob = (own_exp / row_total).astype(jnp.bfloat16)
    mixed_lat = (jnp.einsum("bhl,blc->bhc", past_prob, cache_lat, preferred_element_type=jnp.float32) + own_prob.astype(jnp.float32)[..., None] * new_lat.astype(jnp.float32)[:, None, :]).astype(jnp.bfloat16)
    out_heads = jnp.einsum("bhc,chv->bhv", mixed_lat, w_uv, preferred_element_type=jnp.float32).astype(jnp.bfloat16)
    attn_out = jnp.dot(out_heads.reshape(out_heads.shape[0], -1), w_o, preferred_element_type=jnp.float32)
    resid_rows = (hidden.astype(jnp.float32) + attn_out).astype(jnp.bfloat16)
    return resid_rows, new_lat, new_rope


def solution(mesh):
    row_spec = P(("rep", "g"))
    full_spec = P()
    in_specs = (row_spec, row_spec, row_spec, row_spec, full_spec, full_spec, full_spec, full_spec, full_spec, full_spec, full_spec, full_spec, full_spec, full_spec, full_spec, P(None, "g"), P(None, "g"), P("g", None))

    def local_step(hidden, cache_lat, cache_rope, seq_lens, gain_attn, w_dq, gain_q, w_uq, w_qr, w_dkv, gain_kv, w_uk, w_uv, w_o, gain_mlp, w_gate, w_up, w_down):
        resid_rows, new_lat, new_rope = attention_rows(hidden, cache_lat, cache_rope, seq_lens, gain_attn, w_dq, gain_q, w_uq, w_qr, w_dkv, gain_kv, w_uk, w_uv, w_o)
        mlp_in = rms_norm(resid_rows.astype(jnp.float32), gain_mlp).astype(jnp.bfloat16)
        group_rows = lax.all_gather(mlp_in, "g", axis=0, tiled=True)
        gate_proj = jnp.dot(group_rows, w_gate, preferred_element_type=jnp.float32)
        up_proj = jnp.dot(group_rows, w_up, preferred_element_type=jnp.float32)
        act_vals = (jax.nn.silu(gate_proj) * up_proj).astype(jnp.bfloat16)
        part_sum = jnp.dot(act_vals, w_down, preferred_element_type=jnp.float32).astype(jnp.bfloat16)
        mlp_rows = lax.psum_scatter(part_sum, "g", scatter_dimension=0, tiled=True)
        out_hidden = (resid_rows.astype(jnp.float32) + mlp_rows.astype(jnp.float32)).astype(jnp.bfloat16)
        return out_hidden, new_lat, new_rope

    return jax.shard_map(local_step, mesh=mesh, in_specs=in_specs, out_specs=(row_spec, row_spec, row_spec), check_vma=False)
```

profile of v0, /device:TPU:21, one launch (start us, length us, event | category | flops | bytes accessed | tf_op | source)
XLA Modules:
  0.0 178.1 jit_solution(16009380924011627506)
XLA Ops:
  7.3 0.5 multiply_power_fusion
  7.8 1.5 convert_element_type.104
  9.3 0.7 iota_compare_fusion
  10.0 1.0 fusion.17
  11.1 0.7 convert_element_type.106
  11.8 0.7 convert_element_type.99
  12.5 0.7 convert_element_type.97
  13.1 1.3 convert_element_type.117
  14.4 2.5 %fusion.25 = f32[32,576]{1,0:T(8,128)S(1)} fusion(bf16[2048,576]{0,1:T(8,128)(2,1)} %param.27, bf16[32,2048]{1,0:T(8,128)(2,1)} %param.18, f32[2048]{0:T(1024)S(1)} %convert_element_type.97, f32[32]{0:T(128)S(1)} %add_rsqrt_fusion.3), kind=kOutput, calls=%fused_computation.47 | convolution fusion | flops 75759616 | bytes 2572416 | tf_op jit(solution)/shard_map/dot_general | solution.py:31
  17.0 0.1 multiply_reduce_fusion.2
  17.1 0.8 multiply_reduce_fusion.1
  18.0 0.5 copy-done.3
  18.5 1.0 fusion.33
  19.5 6.5 %fusion.5 = bf16[32,20,512]{2,0,1:T(8,128)(2,1)S(1)} fusion(bf16[512,20,192]{0,2,1:T(8,128)(2,1)} %param.29, bf16[768,20,192]{0,2,1:T(8,128)(2,1)} %param.25, f32[32,768]{1,0:T(8,128)S(1)} %get-tuple-element.14, f32[768]{0:T(1024)S(1)} %convert_element_type.99, f32[32]{0:T(128)S(1)} %add_rsqrt_fusion.2), kind=kOutput, calls=%fused_computation.13 | convolution fusion | flops 315097088 | bytes 10587264 | tf_op jit(solution)/shard_map/bhn,chn->bhc/dot_general | solution.py:34
  26.0 0.5 fusion.10
  26.5 10.2 %fusion.12 = f32[32,20,512]{2,1,0:T(8,128)S(1)} fusion(bf16[32,512,512]{2,1,0:T(8,128)(2,1)} %param.19, bf16[32,20,512]{2,0,1:T(8,128)(2,1)S(1)} %fusion.5), kind=kOutput, calls=%fused_computation.22 | convolution fusion | flops 335544320 | bytes 18743296 | tf_op jit(solution)/shard_map/bhc,blc->bhl/dot_general | solution.py:35
  36.8 0.1 subtract_convert_fusion.1
  37.0 0.2 subtract_convert_fusion
  37.2 0.1 pad_maximum_fusion
  37.3 0.2 fusion.20
  37.5 2.2 %fusion.39 = (f32[32,20]{1,0:T(8,128)S(1)}, f32[32,20,512]{2,1,0:T(8,128)S(1)}) fusion(f32[32,20,512]{2,1,0:T(8,128)S(1)} %fusion.12, bf16[32,512,64]{1,2,0:T(8,128)(2,1)} %param.20, bf16[32,20,64]{2,0,1:T(8,128)(2,1)S(1)} %pad_maximum_fusion, pred[32,512]{1,0:T(8,128)(4,1)S(1)} %iota_compare_fusion), kind=kOutput, calls=%fused_computation.69 | convolution fusion | flops 43253120 | bytes 4819456 | tf_op jit(solution)/shard_map/bhr,blr->bhl/dot_general | solution.py:35
  39.8 0.5 fusion.2
  40.3 8.1 %fusion.7 = f32[32,20,512]{2,1,0:T(8,128)S(1)} fusion(bf16[32,512,512]{2,1,0:T(8,128)(2,1)} %param.19, f32[32,20,512]{2,1,0:T(8,128)S(1)} %get-tuple-element.16, f32[32,20]{1,0:T(8,128)S(1)} %get-tuple-element.10, f32[32,20]{1,0:T(8,128)S(1)} %fusion.31), kind=kOutput, calls=%fused_computation.17 | convolution fusion | flops 336527360 | bytes 19403776 | tf_op jit(solution)/shard_map/bhl,blc->bhc/dot_general | solution.py:45
  48.5 3.7 %fusion.6 = bf16[20,4,8,256]{3,2,1,0:T(8,128)(2,1)S(1)} fusion(bf16[512,20,256]{2,0,1:T(8,128)(2,1)} %param.30, f32[32,20,512]{2,1,0:T(8,128)S(1)} %fusion.7, f32[32,512]{1,0:T(8,128)S(1)} %get-tuple-element.3, f32[32,20]{0,1:T(8,128)S(1)} %copy.26), kind=kOutput, calls=%fused_computation.16 | convolution fusion | flops 168919040 | bytes 6949376 | tf_op jit(solution)/shard_map/bhc,chv->bhv/dot_general | solution.py:46
  52.3 9.3 %multiply_reduce_fusion = (f32[32]{0:T(128)S(1)}, f32[32,2048]{1,0:T(8,128)S(1)}) fusion(bf16[32,5120]{1,0:T(8,128)(2,1)S(1)} %bitcast.34, bf16[5120,2048]{1,0:T(8,128)(2,1)} %param.31, bf16[32,2048]{1,0:T(8,128)(2,1)S(1)} %copy-done.2), kind=kOutput, calls=%fused_computation.35 | convolution fusion | flops 671481856 | bytes 21692544 | tf_op jit(solution)/shard_map/dot_general | solution.py:47
  61.6 0.8 multiply_convert_fusion
  62.5 41.3 %all-gather.2.cloned.1.call-done = bf16[512,2048]{1,0:T(8,128)(2,1)} async-done(((bf16[32,2048]{1,0:T(8,128)(2,1)}), bf16[512,2048]{1,0:T(8,128)(2,1)}) %all-gather.2.cloned.1.call-update) | async-done | bytes 2097168 | tf_op jit(solution)/shard_map/all_gather | solution.py:60
  103.9 4.5 %fusion.40 = f32[512,640]{1,0:T(8,128)} fusion(bf16[512,2048]{1,0:T(8,128)(2,1)} %all-gather.2.cloned.1.call-done, bf16[2048,640]{1,0:T(8,128)(2,1)S(1)} %copy-done.8), kind=kOutput, calls=%fused_computation.70 | convolution fusion | flops 1342177280 | bytes 6029312 | tf_op jit(solution)/shard_map/dot_general | solution.py:61
  108.4 9.0 %convolution_convert_fusion = bf16[512,2048]{1,0:T(8,128)(2,1)} fusion(bf16[640,2048]{1,0:T(8,128)(2,1)} %param.35, bf16[512,2048]{1,0:T(8,128)(2,1)} %all-gather.2.cloned.1.call-done, bf16[2048,640]{1,0:T(8,128)(2,1)} %param.34, f32[512,640]{1,0:T(8,128)} %fusion.40), kind=kOutput, calls=%fused_computation | convolution fusion | flops 2687369216 | bytes 10747904 | tf_op jit(solution)/shard_map/dot_general | solution.py:64
  117.4 0.7 pad_maximum_fusion.1
  118.1 51.6 %reduce-scatter.2.cloned.1.call-done = bf16[32,2048]{1,0:T(8,128)(2,1)} async-done(((bf16[512,2048]{1,0:T(8,128)(2,1)}), bf16[32,2048]{1,0:T(8,128)(2,1)}) %reduce-scatter.2.cloned.1.call-update) | async-done | bytes 131088 | tf_op jit(solution)/shard_map/reduce_scatter | solution.py:65
  169.7 1.6 add_convert_fusion.1
  (31 shorter events, 0.6 us)
Async XLA Ops:
  7.2 9.9 %copy-start = (bf16[2048,768]{1,0:T(8,128)(2,1)S(1)}, bf16[2048,768]{1,0:T(8,128)(2,1)}, u32[]{:S(2)}) copy-start(bf16[2048,768]{1,0:T(8,128)(2,1)} %param.23) | copy-start | bytes 9437188
  7.2 9.9 %copy-start.2 = (bf16[32,2048]{1,0:T(8,128)(2,1)S(1)}, bf16[32,2048]{1,0:T(8,128)(2,1)}, u32[]{:S(2)}) copy-start(bf16[32,2048]{1,0:T(8,128)(2,1)} %param.18) | copy-start | bytes 393220
  7.2 96.7 %all-gather.2.cloned.1.call-start = ((), (), s32[]{:S(2)}) async-start(), calls=%async_computation.1 | async-start | bytes 2228224 | tf_op jit(solution)/shard_map/all_gather | solution.py:60
  17.0 1.6 copy-start.3
  18.0 8.0 %copy-start.5 = (bf16[32,512]{1,0:T(8,128)(2,1)}, bf16[32,512]{1,0:T(8,128)(2,1)S(1)}, u32[]{:S(2)}) copy-start(bf16[32,512]{1,0:T(8,128)(2,1)S(1)} %get-tuple-element.4) | copy-start | bytes 98308
  26.5 10.3 %copy-start.6 = (f32[32]{0:T(128)S(1)}, f32[32]{0:T(128)}, u32[]{:S(2)}) copy-start(f32[32]{0:T(128)} %multiply_power_fusion) | copy-start | bytes 388
  26.5 10.3 %copy-start.7 = (f32[32]{0:T(128)S(1)}, f32[32]{0:T(128)}, u32[]{:S(2)}) copy-start(f32[32]{0:T(128)} %convert_element_type.104) | copy-start | bytes 388
  52.3 9.4 %copy-start.4 = (f32[2048]{0:T(1024)S(1)}, f32[2048]{0:T(1024)}, u32[]{:S(2)}) copy-start(f32[2048]{0:T(1024)} %convert_element_type.117) | copy-start | bytes 24580
  52.3 51.6 %copy-start.8 = (bf16[2048,640]{1,0:T(8,128)(2,1)S(1)}, bf16[2048,640]{1,0:T(8,128)(2,1)}, u32[]{:S(2)}) copy-start(bf16[2048,640]{1,0:T(8,128)(2,1)} %param.33) | copy-start | bytes 7864324
  62.4 107.3 %reduce-scatter.2.cloned.1.call-start = ((), (), s32[]{:S(2)}) async-start(), calls=%async_computation.2 | async-start | bytes 2228224 | tf_op jit(solution)/shard_map/reduce_scatter | solution.py:65
  108.4 62.9 %copy-start.1 = (bf16[2048,768]{1,0:T(8,128)(2,1)S(1)}, bf16[2048,768]{1,0:T(8,128)(2,1)}, u32[]{:S(2)}) copy-start(bf16[2048,768]{1,0:T(8,128)(2,1)} %param.23) | copy-start | bytes 9437188
Sparse Core Ops, SparseCore 0:
  62.6 41.2 all-gather.1
  117.5 52.1 reduce-scatter.1
where the time goes:
time: 180 us; the launch traced here: 178 us
  waiting for transfers between devices  93.1 us (52%)
  matrix products  58.7 us (33%)
  between operations  14.2 us (8%)
  other arithmetic  11.4 us (6%)
    reduce_scatter x1, waiting for transfers between devices, local_step(): mlp_rows = lax.psum_scatter(part_sum, 'g', scatter_dimension=0, tiled=True)  51.6 us
    all_gather x1, waiting for transfers between devices, local_step(): group_rows = lax.all_gather(mlp_in, 'g', axis=0, tiled=True)  41.3 us
    dot_general x1, matrix products, attention_rows(): jnp.einsum('bhc,blc->bhl', q_abs, cache_lat, preferred_element_type=jnp.f...  10.2 us
    dot_general x1, matrix products, attention_rows(): jnp.dot(out_heads.reshape(out_heads.shape[0], -1), w_o, preferred_element...  9.34 us
    dot_general x1, matrix products, local_step(): jnp.dot(act_vals, w_down, preferred_element_type=jnp.float32)  8.98 us
    dot_general x1, matrix products, attention_rows(): jnp.einsum('bhl,blc->bhc', past_prob, cache_lat, preferred_element_type=j...  8.14 us
    dot_general x1, matrix products, attention_rows(): jnp.einsum('bhn,chn->bhc', q_nope, w_uk, preferred_element_type=jnp.float32)  6.48 us
    dot_general x1, matrix products, local_step(): gate_proj = jnp.dot(group_rows, w_gate, preferred_element_type=jnp.float32)  4.49 us
  transfers between devices with their start and end apart: 2, of which 2 were waited for; matrix products, arithmetic and copies ran while one was open for 0% of the time, Pallas kernels for 0%

commit v1 on v0

--- a/solution.py
+++ b/solution.py
@@ -1,6 +1,10 @@
+import functools
+
 import jax
 import jax.numpy as jnp
 from jax import lax
+from jax.experimental import pallas as pl
+from jax.experimental.pallas import tpu as pltpu
 from jax.sharding import PartitionSpec as P
 
 
@@ -48,6 +52,201 @@
     resid_rows = (hidden.astype(jnp.float32) + attn_out).astype(jnp.bfloat16)
     return resid_rows, new_lat, new_rope
 
+MESH = pl.DeviceIdType.MESH
+COL_PARTS = 2
+
+
+def mlp_kernel(n, resid_ref, gain_ref, wg_ref, wu_ref, wd_ref, out_ref, wgu, wdn, ag, y_own, y_snd, y_rcv, f_snd, b_snd, f_rcv, b_rcv,
+               w_sem, agf_s, agf_r, agb_s, agb_r, agd_s, agd_r, yd_s, yd_r, rsf_s, rsf_r, rsb_s, rsb_r):
+    me = lax.axis_index("g")
+    chips = n // 2
+    far = chips // 2
+    rows, dim = resid_ref.shape
+    ff = wg_ref.shape[1]
+    chip, core = me // 2, lax.rem(me, 2)
+    nxt = {"g": lax.rem(chip + 1, chips) * 2 + core}
+    prv = {"g": lax.rem(chip + chips - 1, chips) * 2 + core}
+    mate = {"g": chip * 2 + (1 - core)}
+
+    weights = [
+        pltpu.make_async_copy(wg_ref, wgu.at[:, 0:ff], w_sem.at[0]),
+        pltpu.make_async_copy(wu_ref, wgu.at[:, ff:2 * ff], w_sem.at[1]),
+        pltpu.make_async_copy(wd_ref, wdn, w_sem.at[2]),
+    ]
+    for copy in weights:
+        copy.start()
+
+    barrier = pltpu.get_barrier_semaphore()
+    for peer in (nxt, prv, mate):
+        pl.semaphore_signal(barrier, inc=1, device_id=peer, device_id_type=MESH)
+
+    resid = resid_ref[...].astype(jnp.float32)
+    mean_sq = jnp.mean(jnp.square(resid), axis=-1, keepdims=True)
+    ag[0, 0:rows, :] = (resid * lax.rsqrt(mean_sq + 1e-6) * gain_ref[...].astype(jnp.float32)).astype(jnp.bfloat16)
+    pl.semaphore_wait(barrier, 3)
+
+    half = rows // 2
+    cols = dim // COL_PARTS
+    parts = [(h, c) for h in range(2) for c in range(COL_PARTS)]
+    fwd_parts = [j for j, (h, c) in enumerate(parts) if h == 0]
+    bwd_parts = [j for j, (h, c) in enumerate(parts) if h == 1]
+
+    def before(k):
+        return 0 if k == 0 else (chips - 1 if k == far else 2 * k - 1)
+
+    def after(k):
+        return 0 if k == 0 else (chips - 1 if k == far else 2 * k)
+
+    def piece(j):
+        h, c = parts[j]
+        return pl.ds(h * half, half), pl.ds(c * cols, cols)
+
+    def remote(src, dst, send, recv, peer):
+        return pltpu.make_async_remote_copy(src_ref=src, dst_ref=dst, send_sem=send, recv_sem=recv, device_id=peer, device_id_type=MESH)
+
+    def gather_fwd(k, j):
+        r, c = piece(j)
+        return remote(ag.at[before(k), r, c], ag.at[before(k + 1), r, c], agf_s.at[k, j], agf_r.at[k, j], nxt)
+
+    def gather_bwd(k, j):
+        r, c = piece(j)
+        return remote(ag.at[after(k), r, c], ag.at[after(k + 1), r, c], agb_s.at[k, j], agb_r.at[k, j], prv)
+
+    def gather_mate(p, h):
+        src, dst = (pl.ds(0, rows), pl.ds(rows, rows)) if h is None else (pl.ds(h * half, half), pl.ds(rows + h * half, half))
+        i = 0 if h is None else h
+        return remote(ag.at[p, src, :], ag.at[p, dst, :], agd_s.at[p, i], agd_r.at[p, i], mate)
+
+    def send_mate_sums(p):
+        return remote(y_snd.at[p], y_rcv.at[p], yd_s.at[p], yd_r.at[p], mate)
+
+    def reduce_fwd(k, j):
+        r, c = piece(j)
+        return remote(f_snd.at[k - 1, r, c], f_rcv.at[k - 1, r, c], rsf_s.at[k - 1, j], rsf_r.at[k - 1, j], nxt)
+
+    def reduce_bwd(k, j):
+        r, c = piece(j)
+        return remote(b_snd.at[k - 1, r, c], b_rcv.at[k - 1, r, c], rsb_s.at[k - 1, j], rsb_r.at[k - 1, j], prv)
+
+    started = []
+
+    def start(copy):
+        copy.start()
+        started.append(copy)
+
+    def compute(first, count):
+        x = ag[first:first + count].reshape(count * 2 * rows, dim)
+        gate_up = jnp.dot(x, wgu[...], preferred_element_type=jnp.float32)
+        act = (jax.nn.silu(gate_up[:, 0:ff]) * gate_up[:, ff:2 * ff]).astype(jnp.bfloat16)
+        y = jnp.dot(act, wdn[...], preferred_element_type=jnp.float32)
+        for i in range(count):
+            y_own[first + i] = y[2 * i * rows:(2 * i + 1) * rows]
+            y_snd[first + i] = y[(2 * i + 1) * rows:(2 * i + 2) * rows]
+            start(send_mate_sums(first + i))
+
+    for j in range(len(parts)):
+        start(gather_fwd(0, j))
+        start(gather_bwd(0, j))
+    start(gather_mate(0, None))
+    for copy in weights:
+        copy.wait()
+    for k in range(1, far + 1):
+        for j in range(len(parts)):
+            if k < far or j in fwd_parts:
+                gather_fwd(k - 1, j).wait_recv()
+                if k < far - 1 or (k == far - 1 and j in fwd_parts):
+                    start(gather_fwd(k, j))
+            if k < far or j in bwd_parts:
+                gather_bwd(k - 1, j).wait_recv()
+                if k < far - 1 or (k == far - 1 and j in bwd_parts):
+                    start(gather_bwd(k, j))
+        if k < far:
+            start(gather_mate(before(k), None))
+            start(gather_mate(after(k), None))
+        else:
+            start(gather_mate(chips - 1, 0))
+            start(gather_mate(chips - 1, 1))
+        if k == 1:
+            gather_mate(0, None).wait_recv()
+            compute(0, 1)
+        else:
+            gather_mate(before(k - 1), None).wait_recv()
+            gather_mate(after(k - 1), None).wait_recv()
+            compute(before(k - 1), 2)
+    gather_mate(chips - 1, 0).wait_recv()
+    gather_mate(chips - 1, 1).wait_recv()
+    compute(chips - 1, 1)
+
+    def pair_sum(p, j):
+        r, c = piece(j)
+        return y_own[p, r, c] + y_rcv[p, r, c]
+
+    for k in range(far, 0, -1):
+        fp, bp = after(k), before(k)
+        send_mate_sums(fp).wait_recv()
+        if bp != fp:
+            send_mate_sums(bp).wait_recv()
+        for j in range(len(parts)):
+            r, c = piece(j)
+            if k < far or j in fwd_parts:
+                total = pair_sum(fp, j)
+                if k < far - 1 or (k == far - 1 and j in fwd_parts):
+                    reduce_fwd(k + 1, j).wait_recv()
+                    total = total + f_rcv[k, r, c].astype(jnp.float32)
+                f_snd[k - 1, r, c] = total.astype(jnp.bfloat16)
+                start(reduce_fwd(k, j))
+            if k < far or j in bwd_parts:
+                total = pair_sum(bp, j)
+                if k < far - 1 or (k == far - 1 and j in bwd_parts):
+                    reduce_bwd(k + 1, j).wait_recv()
+                    total = total + b_rcv[k, r, c].astype(jnp.float32)
+                b_snd[k - 1, r, c] = total.astype(jnp.bfloat16)
+                start(reduce_bwd(k, j))
+    send_mate_sums(0).wait_recv()
+    for j in range(len(parts)):
+        r, c = piece(j)
+        reduce_fwd(1, j).wait_recv()
+        reduce_bwd(1, j).wait_recv()
+        total = pair_sum(0, j) + f_rcv[0, r, c].astype(jnp.float32) + b_rcv[0, r, c].astype(jnp.float32)
+        out_ref[r, c] = (resid_ref[r, c].astype(jnp.float32) + total).astype(jnp.bfloat16)
+    for copy in started:
+        copy.wait_send()
+
+
+def mlp_block(n, resid_rows, gain_mlp, w_gate, w_up, w_down):
+    rows, dim = resid_rows.shape
+    ff = w_gate.shape[1]
+    chips = n // 2
+    far = chips // 2
+    parts = 2 * COL_PARTS
+    vmem, dma = pltpu.VMEM, pltpu.SemaphoreType.DMA
+    wide, narrow = jnp.float32, jnp.bfloat16
+    return pl.pallas_call(
+        functools.partial(mlp_kernel, n),
+        out_shape=jax.ShapeDtypeStruct((rows, dim), narrow),
+        in_specs=[pl.BlockSpec(memory_space=pltpu.VMEM)] * 2 + [pl.BlockSpec(memory_space=pl.ANY)] * 3,
+        out_specs=pl.BlockSpec(memory_space=pltpu.VMEM),
+        scratch_shapes=[
+            vmem((dim, 2 * ff), narrow),
+            vmem((ff, dim), narrow),
+            vmem((chips, 2 * rows, dim), narrow),
+            vmem((chips, rows, dim), wide),
+            vmem((chips, rows, dim), wide),
+            vmem((chips, rows, dim), wide),
+            vmem((far, rows, dim), narrow),
+            vmem((far, rows, dim), narrow),
+            vmem((far, rows, dim), narrow),
+            vmem((far, rows, dim), narrow),
+            dma((3,)),
+            dma((far, parts)), dma((far, parts)), dma((far, parts)), dma((far, parts)),
+            dma((chips, 2)), dma((chips, 2)), dma((chips,)), dma((chips,)),
+            dma((far, parts)), dma((far, parts)), dma((far, parts)), dma((far, parts)),
+        ],
+        compiler_params=pltpu.CompilerParams(collective_id=0, has_side_effects=True),
+        cost_estimate=pl.CostEstimate(flops=6 * n * rows * dim * ff, bytes_accessed=6 * dim * ff, transcendentals=0),
+        name="mlp_ring",
+    )(resid_rows, gain_mlp.reshape(1, dim), w_gate, w_up, w_down)
+
 
 def solution(mesh):
     row_spec = P(("rep", "g"))
@@ -56,14 +255,7 @@
 
     def local_step(hidden, cache_lat, cache_rope, seq_lens, gain_attn, w_dq, gain_q, w_uq, w_qr, w_dkv, gain_kv, w_uk, w_uv, w_o, gain_mlp, w_gate, w_up, w_down):
         resid_rows, new_lat, new_rope = attention_rows(hidden, cache_lat, cache_rope, seq_lens, gain_attn, w_dq, gain_q, w_uq, w_qr, w_dkv, gain_kv, w_uk, w_uv, w_o)
-        mlp_in = rms_norm(resid_rows.astype(jnp.float32), gain_mlp).astype(jnp.bfloat16)
-        group_rows = lax.all_gather(mlp_in, "g", axis=0, tiled=True)
-        gate_proj = jnp.dot(group_rows, w_gate, preferred_element_type=jnp.float32)
-        up_proj = jnp.dot(group_rows, w_up, preferred_element_type=jnp.float32)
-        act_vals = (jax.nn.silu(gate_proj) * up_proj).astype(jnp.bfloat16)
-        part_sum = jnp.dot(act_vals, w_down, preferred_element_type=jnp.float32).astype(jnp.bfloat16)
-        mlp_rows = lax.psum_scatter(part_sum, "g", scatter_dimension=0, tiled=True)
-        out_hidden = (resid_rows.astype(jnp.float32) + mlp_rows.astype(jnp.float32)).astype(jnp.bfloat16)
+        out_hidden = mlp_block(mesh.shape["g"], resid_rows, gain_mlp, w_gate, w_up, w_down)
         return out_hidden, new_lat, new_rope
 
     return jax.shard_map(local_step, mesh=mesh, in_specs=in_specs, out_specs=(row_spec, row_spec, row_spec), check_vma=False)

time: 180 us -> 104 us (0.58); the launches traced: 178 us -> 104 us
  waiting for transfers between devices: 93.1 us -> 0 us
  Pallas kernels: 0 us -> 46.6 us
  between operations: 14.2 us -> 0.78 us
  matrix products: 58.7 us -> 46.2 us
  other arithmetic: 11.4 us -> 7.38 us
  local copies, waits for them, and re-layouts: 0.68 us -> 3.01 us
    reduce_scatter x1 -> x0, waiting for transfers between devices: 51.6 us -> none  [local_step(): mlp_rows = lax.psum_scatter(part_sum, 'g', scatter_dimension=0, tiled=True)]
    pallas_call x0 -> x1, Pallas kernels: none -> 46.6 us  [mlp_block(): pl.pallas_call(functools.partial(mlp_kernel, n), out_shape=jax.ShapeDtype...]
    all_gather x1 -> x0, waiting for transfers between devices: 41.3 us -> none  [local_step(): group_rows = lax.all_gather(mlp_in, 'g', axis=0, tiled=True)]
    dot_general x2 -> x0, matrix products: 13.5 us -> none  [the longest x1 8.98 us: local_step(): jnp.dot(act_vals, w_down, preferred_element_type=jnp.float32)]
    convert_element_type x2 -> x0, other arithmetic: 2.33 us -> none  [the longest x1 1.58 us: local_step(): (resid_rows.astype(jnp.float32) + mlp_rows.astype(jnp.float32)).astype(jn...]
  transfers between devices with their start and end apart: 2 -> 0, of which waited for: 2 -> 0; matrix products, arithmetic and copies ran while one was open for 0% -> 0% of each run, Pallas kernels for 0% -> 0%
where the time goes in v1:
time: 104 us
  Pallas kernels  46.6 us (45%)
  matrix products  46.2 us (44%)
  other arithmetic  7.38 us (7%)
  local copies, waits for them, and re-layouts  3.01 us (3%)
    pallas_call x1, Pallas kernels, mlp_block(): pl.pallas_call(functools.partial(mlp_kernel, n), out_shape=jax.ShapeDtype...  46.6 us
    dot_general x1, matrix products, attention_rows(): jnp.einsum('bhc,blc->bhl', q_abs, cache_lat, preferred_element_type=jnp.f...  10.2 us
    dot_general x1, matrix products, attention_rows(): jnp.dot(out_heads.reshape(out_heads.shape[0], -1), w_o, preferred_element...  9.74 us
    dot_general x1, matrix products, attention_rows(): jnp.einsum('bhl,blc->bhc', past_prob, cache_lat, preferred_element_type=j...  8.18 us
    dot_general x1, matrix products, attention_rows(): jnp.einsum('bhn,chn->bhc', q_nope, w_uk, preferred_element_type=jnp.float32)  6.48 us
    dot_general x1, matrix products, attention_rows(): jnp.einsum('bhc,chv->bhv', mixed_lat, w_uv, preferred_element_type=jnp.fl...  3.73 us
    dot_general x1, matrix products, attention_rows(): kv_raw = jnp.dot(normed, w_dkv, preferred_element_type=jnp.float32)  2.53 us
    dot_general x1, matrix products, attention_rows(): jnp.einsum('bhr,blr->bhl', q_rope, cache_rope, preferred_element_type=jnp...  2.23 us

profile of v1, /device:TPU:21, one launch (start us, length us, event | category | flops | bytes accessed | tf_op | source)
XLA Modules:
  0.0 104.0 jit_solution(9578197747987870390)
XLA Ops:
  0.6 0.0 copy-start
  0.7 0.8 convert_element_type.82
  1.5 1.2 %fusion.15 = f32[32]{0:T(128)S(1)} fusion(bf16[32,2048]{1,0:T(8,128)(2,1)} %param.18), kind=kLoop, calls=%fused_computation.26 | loop fusion | flops 196576 | bytes 131200 | tf_op jit(solution)/shard_map/reduce_sum | solution.py:12
  2.7 0.7 convert_element_type.84
  3.4 0.7 convert_element_type.77
  4.1 0.7 convert_element_type.75
  4.8 1.3 %reshape.136.gain_ref = bf16[1,2048]{1,0:T(2,128)(2,1)} reshape(bf16[2048]{0:T(1024)(128)(2,1)} %param.32) | data formatting | bytes 8192 | tf_op jit(solution)/shard_map/reshape | solution.py:248
  6.1 0.7 iota_compare_fusion
  6.8 2.5 %fusion.23 = f32[32,576]{1,0:T(8,128)S(1)} fusion(bf16[2048,576]{0,1:T(8,128)(2,1)} %param.27, bf16[32,2048]{1,0:T(8,128)(2,1)} %param.18, f32[2048]{0:T(1024)S(1)} %convert_element_type.75, f32[32]{0:T(128)S(1)} %add_rsqrt_fusion.2), kind=kOutput, calls=%fused_computation.40 | convolution fusion | flops 75759616 | bytes 2572416 | tf_op jit(solution)/shard_map/dot_general | solution.py:35
  9.3 0.1 multiply_reduce_fusion.1
  9.5 0.1 subtract_convert_fusion.1
  9.6 0.1 fusion.48
  9.7 0.7 pad_maximum_fusion.1
  10.4 0.7 fusion.35
  11.1 0.8 multiply_reduce_fusion
  11.9 1.0 fusion.30
  12.9 0.2 subtract_convert_fusion
  13.1 0.1 pad_maximum_fusion
  13.2 0.8 fusion.18
  14.1 6.5 %fusion.3 = bf16[32,20,512]{2,0,1:T(8,128)(2,1)S(1)} fusion(bf16[512,20,192]{0,2,1:T(8,128)(2,1)} %param.29, bf16[768,20,192]{0,2,1:T(8,128)(2,1)} %param.25, f32[32,768]{1,0:T(8,128)S(1)} %get-tuple-element.14, f32[768]{0:T(1024)} %copy-done.6, f32[32]{0:T(128)S(1)} %add_rsqrt_fusion.1), kind=kOutput, calls=%fused_computation.9 | convolution fusion | flops 315097088 | bytes 10587264 | tf_op jit(solution)/shard_map/bhn,chn->bhc/dot_general | solution.py:38
  20.5 0.0 copy-done.7
  20.6 0.5 fusion.8
  21.0 10.2 %fusion.10 = f32[32,20,512]{2,1,0:T(8,128)S(1)} fusion(bf16[32,512,512]{2,1,0:T(8,128)(2,1)} %param.19, bf16[32,20,512]{2,0,1:T(8,128)(2,1)S(1)} %fusion.3), kind=kOutput, calls=%fused_computation.18 | convolution fusion | flops 335544320 | bytes 18743296 | tf_op jit(solution)/shard_map/bhc,blc->bhl/dot_general | solution.py:39
  31.3 2.2 %fusion.36 = (f32[32,20]{1,0:T(8,128)S(1)}, f32[32,20,512]{2,1,0:T(8,128)S(1)}) fusion(f32[32,20,512]{2,1,0:T(8,128)S(1)} %fusion.10, bf16[32,512,64]{1,2,0:T(8,128)(2,1)} %param.20, bf16[32,20,64]{2,0,1:T(8,128)(2,1)S(1)} %pad_maximum_fusion, pred[32,512]{1,0:T(8,128)(4,1)S(1)} %iota_compare_fusion), kind=kOutput, calls=%fused_computation.60 | convolution fusion | flops 43253120 | bytes 4819456 | tf_op jit(solution)/shard_map/bhr,blr->bhl/dot_general | solution.py:39
  33.5 0.5 fusion.1
  34.0 0.0 copy-start.4
  34.0 8.2 %fusion.5 = f32[32,20,512]{2,1,0:T(8,128)S(1)} fusion(bf16[32,512,512]{2,1,0:T(8,128)(2,1)} %param.19, f32[32,20,512]{2,1,0:T(8,128)S(1)} %get-tuple-element.16, f32[32,20]{1,0:T(8,128)S(1)} %get-tuple-element.10, f32[32,20]{1,0:T(8,128)S(1)} %fusion.29), kind=kOutput, calls=%fused_computation.13 | convolution fusion | flops 336527360 | bytes 19403776 | tf_op jit(solution)/shard_map/bhl,blc->bhc/dot_general | solution.py:49
  42.2 0.1 copy.26
  42.3 3.7 %fusion.4 = bf16[20,4,8,256]{3,2,1,0:T(8,128)(2,1)S(1)} fusion(bf16[512,20,256]{2,0,1:T(8,128)(2,1)} %param.30, f32[32,20,512]{2,1,0:T(8,128)S(1)} %fusion.5, f32[32,512]{1,0:T(8,128)S(1)} %copy-done.4, f32[32,20]{0,1:T(8,128)S(1)} %copy.26), kind=kOutput, calls=%fused_computation.12 | convolution fusion | flops 168919040 | bytes 6949376 | tf_op jit(solution)/shard_map/bhc,chv->bhv/dot_general | solution.py:50
  46.1 9.7 %fusion.resid_ref = bf16[32,2048]{1,0:T(8,128)(2,1)} fusion(bf16[32,5120]{1,0:T(8,128)(2,1)S(1)} %bitcast.29, bf16[5120,2048]{1,0:T(8,128)(2,1)} %param.31, bf16[32,2048]{1,0:T(8,128)(2,1)S(1)} %copy-done.2), kind=kOutput, calls=%fused_computation.1 | convolution fusion | flops 671285248 | bytes 21561344 | tf_op jit(solution)/shard_map/dot_general | solution.py:51
  55.8 46.6 %mlp_ring.1 = bf16[32,2048]{1,0:T(8,128)(2,1)} custom-call(bf16[32,2048]{1,0:T(8,128)(2,1)} %fusion.resid_ref, bf16[1,2048]{1,0:T(2,128)(2,1)} %reshape.136.gain_ref, bf16[2048,640]{1,0:T(8,128)(2,1)} %wg_ref.1, bf16[2048,640]{1,0:T(8,128)(2,1)} %wu_ref.1, bf16[640,2048]{1,0:T(8,128)(2,1)} %wd_ref.1), custom_call_target="tpu_custom_call" | custom-call | flops 4026531840 | bytes 7864320 | tf_op jit(solution)/shard_map/mlp_ring/pallas_call | solution.py:224
  102.4 1.6 %copy.53 = bf16[32,2048]{1,0:T(8,128)(2,1)} copy(bf16[32,2048]{1,0:T(8,128)(2,1)} %mlp_ring.1) | data formatting | bytes 262144
  (20 shorter events, 0.1 us)
Async XLA Ops:
  0.6 10.5 %copy-start = (bf16[2048,768]{1,0:T(8,128)(2,1)S(1)}, bf16[2048,768]{1,0:T(8,128)(2,1)}, u32[]{:S(2)}) copy-start(bf16[2048,768]{1,0:T(8,128)(2,1)} %param.23) | copy-start | bytes 9437188
  0.6 10.5 %copy-start.2 = (bf16[32,2048]{1,0:T(8,128)(2,1)S(1)}, bf16[32,2048]{1,0:T(8,128)(2,1)}, u32[]{:S(2)}) copy-start(bf16[32,2048]{1,0:T(8,128)(2,1)} %param.18) | copy-start | bytes 393220
  4.1 7.8 %copy-start.6 = (f32[768]{0:T(1024)}, f32[768]{0:T(1024)S(1)}, u32[]{:S(2)}) copy-start(f32[768]{0:T(1024)S(1)} %convert_element_type.77) | copy-start | bytes 9220
  9.3 2.6 %copy-start.3 = (bf16[768,20,64]{0,2,1:T(8,128)(2,1)S(1)}, bf16[768,20,64]{0,2,1:T(8,128)(2,1)}, u32[]{:S(2)}) copy-start(bf16[768,20,64]{0,2,1:T(8,128)(2,1)} %param.26) | copy-start | bytes 5898244
  14.1 6.5 %copy-start.7 = (bf16[32,512]{1,0:T(8,128)(2,1)S(1)}, bf16[32,512]{1,0:T(8,128)(2,1)}, u32[]{:S(2)}) copy-start(bf16[32,512]{1,0:T(8,128)(2,1)} %get-tuple-element.21) | copy-start | bytes 98308
  31.3 2.2 %copy-start.5 = (f32[32,1,20]{2,1,0:T(1,128)S(1)}, f32[32,1,20]{2,1,0:T(1,128)}, u32[]{:S(2)}) copy-start(f32[32,1,20]{2,1,0:T(1,128)} %fusion.18) | copy-start | bytes 7684
  34.0 8.3 %copy-start.4 = (f32[32,512]{1,0:T(8,128)S(1)}, f32[32,512]{1,0:T(8,128)}, u32[]{:S(2)}) copy-start(f32[32,512]{1,0:T(8,128)} %get-tuple-element.3) | copy-start | bytes 196612
  55.8 48.2 %copy-start.1 = (bf16[2048,768]{1,0:T(8,128)(2,1)S(1)}, bf16[2048,768]{1,0:T(8,128)(2,1)}, u32[]{:S(2)}) copy-start(bf16[2048,768]{1,0:T(8,128)(2,1)} %param.23) | copy-start | bytes 9437188
